TPU v7x, 128 devices: a whole 4x4x4 slice. The times are simulated.
128 devices in a mesh: row: 8 (over z, core), col: 16 (over y, x).
Axes of the slice: x: 4, y: 4, z: 4, core: 2. Of those that a mesh axis runs over, the one named last changes fastest.
Arguments:
- grad_out: bfloat16 [131072, 256], P(('row', 'col')), may hold values from -6 to 6
- rel_weight: bfloat16 [4, 256, 256], replicated, may hold values from -0.375 to 0.375
- adjacency: bfloat16 [24576, 128, 128], P(('row', 'col')), may hold values from -0.5 to 0.5
- block_row: int32 [24576], P(('row', 'col')), may hold values from 0 to 127, as said below
- block_col: int32 [24576], P(('row', 'col')), may hold values from 0 to 63
- type_count: int32 [512], P(('row', 'col')), may hold values from 0 to 192, as said below
Outputs:
- grad_in: float32 [131072, 256], P(('row', 'col'))
Inputs may be any that keep to these rules, and one draw needn't show every extreme that they name: `block_row`: among all 192 slots of one tile, at most 4 distinct values fall in any aligned range of 8 values (the node blocks of one device of the tile row), and in every tile some range holds exactly 4. `type_count`: A tile's 4 counts sum to at most 192; in some tile a single type holds all 192 slots.
All inputs are finite; a program needn't handle non-finite values.
Results may differ from a plain program's by a relative error of at most 0.012.
Values may be sent and summed in bfloat16 or wider, within the bound.
A program may use at most 192 MiB of HBM per device.

v0:
```python
import math
import jax
import jax.numpy as jnp
from jax import lax
from jax.sharding import PartitionSpec as P


def per_device(grad_out, rel_weight, adjacency, block_row, block_col, type_count):
    ncols = lax.axis_size("col")
    nrows = lax.axis_size("row")
    blk = adjacency.shape[1]
    feat = grad_out.shape[1]
    kinds = rel_weight.shape[0]
    owned = grad_out.shape[0] // blk
    slots_total = adjacency.shape[0]
    wcat = jnp.transpose(rel_weight, (2, 0, 1)).reshape(feat, kinds * feat)
    gathered = jnp.dot(
        lax.all_gather(grad_out, "col", axis=0, tiled=True),
        wcat,
        preferred_element_type=jnp.float32,
    ).astype(jnp.bfloat16)
    table = gathered.reshape(ncols * owned, blk, kinds, feat)
    ends = jnp.cumsum(type_count)
    total = ends[kinds - 1]
    position = jnp.arange(slots_total, dtype=jnp.int32)
    kind = jnp.minimum(
        jnp.sum((position[:, None] >= ends[None, :]).astype(jnp.int32), axis=1), kinds - 1
    )
    live = position < total
    group = math.gcd(slots_total, 64)
    groups = slots_total // group
    partial_start = jnp.zeros((nrows * owned, blk, feat), jnp.float32)

    def step(index, partial_value):
        start = index * group
        adj_part = lax.dynamic_slice_in_dim(adjacency, start, group, 0)
        slot_part = lax.dynamic_slice_in_dim(block_row, start, group, 0)
        kind_part = lax.dynamic_slice_in_dim(kind, start, group, 0)
        live_part = lax.dynamic_slice_in_dim(live, start, group, 0)
        col_part = lax.dynamic_slice_in_dim(block_col, start, group, 0)
        picked = table[slot_part, :, kind_part, :]
        term = jnp.einsum("kab,kaf->kbf", adj_part, picked, preferred_element_type=jnp.float32)
        term = jnp.where(live_part[:, None, None], term, jnp.float32(0.0))
        return partial_value.at[col_part].add(term)

    partial_value = lax.fori_loop(0, groups, step, partial_start)
    return lax.psum_scatter(
        partial_value.reshape(nrows * owned * blk, feat).astype(jnp.bfloat16),
        "row",
        scatter_dimension=0,
        tiled=True,
    ).astype(jnp.float32)


def solution(mesh):
    in_specs = (
        P(("row", "col"), None),
        P(),
        P(("row", "col"), None, None),
        P(("row", "col")),
        P(("row", "col")),
        P(("row", "col")),
    )
    out_specs = P(("row", "col"), None)
    return jax.shard_map(
        per_device, mesh=mesh, in_specs=in_specs, out_specs=out_specs, check_vma=False
    )
```

profile of v0, /device:TPU:0, one launch (start us, length us, event | category | flops | bytes accessed | tf_op | source)
XLA Modules:
  0.0 332.7 jit_solution(6268306720380920505)
XLA Ops:
  6.5 0.0 copy-start
  6.5 0.0 all-gather.2.cloned.1.call-start
  6.5 0.7 all-gather.2.cloned.1.call-update
  7.3 0.0 reduce-scatter.2.cloned.1.call-start
  7.3 0.8 reduce-window.4
  8.1 0.6 slice.4
  8.7 0.6 iota_compare_fusion.1
  9.3 0.1 convert_reduce_fusion
  9.4 73.3 %all-gather.2.cloned.1.call-done = bf16[16384,256]{1,0:T(8,128)(2,1)} async-done(((bf16[1024,256]{1,0:T(8,128)(2,1)}), bf16[16384,256]{1,0:T(8,128)(2,1)}) %all-gather.2.cloned.1.call-update) | async-done | bytes 8388624 | tf_op jit(solution)/shard_map/all_gather | solution.py:18
  82.7 0.0 copy-done
  82.7 17.5 %convolution_convert_fusion = bf16[16384,1024]{1,0:T(8,128)(2,1)} fusion(bf16[16384,256]{1,0:T(8,128)(2,1)} %all-gather.2.cloned.1.call-done, bf16[256,1024]{0,1:T(8,128)(2,1)S(1)} %bitcast.12), kind=kOutput, calls=%fused_computation.13 | convolution fusion | flops 8606711808 | bytes 42467328 | tf_op jit(solution)/shard_map/dot_general | solution.py:17
  100.1 54.7 %reshape.19 = bf16[128,128,4,256]{3,2,1,0:T(4,128)(2,1)} reshape(bf16[16384,1024]{1,0:T(8,128)(2,1)} %convolution_convert_fusion) | data formatting | bytes 67108864 | tf_op jit(solution)/shard_map/reshape | solution.py:22
  154.8 23.0 %copy.12 = bf16[128,128,4,256]{3,1,2,0:T(8,128)(2,1)} copy(bf16[128,128,4,256]{3,2,1,0:T(4,128)(2,1)} %reshape.19) | data formatting | bytes 67108864 | tf_op jit(solution)/shard_map/while | solution.py:46
  177.9 0.0 copy-start.2
  177.9 0.0 copy-start.3
  177.9 4.2 %broadcast_in_dim.53 = f32[64,128,256]{2,1,0:T(8,128)} broadcast(f32[]{:T(128)} %constant.55.clone.1), dimensions={} | broadcast | bytes 8388612 | tf_op jit(solution)/shard_map/broadcast_in_dim | solution.py:32
  182.1 0.0 copy-done.2
  182.1 0.0 copy-done.3
  182.1 97.6 %while.13 = (s32[]{:T(128)}, f32[64,128,256]{2,1,0:T(8,128)}, s32[192]{0:T(256)S(1)}, pred[192]{0:T(512)(128)(4,1)S(1)}, bf16[192,128,128]{2,1,0:T(8,128)(2,1)},...) while((s32[]{:T(128)}, f32[64,128,256]{2,1,0:T(8,128)}, ...), condition=%wide.region_4.5_spmd, body=%wide.region_2.4_spmd.sunk | while | flops 541066112 | bytes 48236912 | solution.py:46
  182.1 0.1 compare_select_fusion.4
  182.2 5.2 %gather_fusion = bf16[64,128,256]{2,1,0:T(8,128)(2,1)} fusion(bf16[128,128,4,256]{3,1,2,0:T(8,128)(2,1)} %get-tuple-element.271, s32[64]{0:T(128)S(1)} %get-tuple-element.239), kind=kCustom, calls=%fused_computation.clone.1 | custom fusion | bytes 8389120 | tf_op jit(solution)/shard_map/while/body/eval_jaxpr/gather | solution.py:41
  187.3 0.1 dynamic_slice.45
  187.4 7.6 %broadcast_select_fusion.2 = f32[64,128,256]{2,1,0:T(8,128)} fusion(pred[64]{0:T(512)(128)(4,1)S(1)} %dynamic_slice.45, bf16[64,128,256]{2,1,0:T(8,128)(2,1)} %gather_fusion, bf16[192,128,128]{2,1,0:T(8,128)(2,1)} %get-tuple-element.268, s32[]{:T(128)S(6)} %select_n.61), kind=kOutput, calls=%fused_computation.2.clone.1 | convolution fusion | flops 538968064 | bytes 14680132 | tf_op jit(solution)/shard_map/while/body/eval_jaxpr/kab,kaf->kbf/dot_general | solution.py:42
  195.0 19.6 %scatter_fusion = f32[64,128,256]{2,1,0:T(8,128)} fusion(f32[64,128,256]{2,1,0:T(8,128)} %get-tuple-element.253, s32[64]{0:T(128)S(1)} %get-tuple-element.238, f32[64,128,256]{2,1,0:T(8,128)} %broadcast_select_fusion.2), kind=kCustom, calls=%fused_computation.1.clone.1 | custom fusion | flops 2097152 | bytes 25166080 | tf_op jit(solution)/shard_map/while/body/eval_jaxpr/scatter-add | solution.py:44
  214.6 0.1 compare_select_fusion.4
  214.7 5.4 %gather_fusion = bf16[64,128,256]{2,1,0:T(8,128)(2,1)} fusion(bf16[128,128,4,256]{3,1,2,0:T(8,128)(2,1)} %get-tuple-element.271, s32[64]{0:T(128)S(1)} %get-tuple-element.239), kind=kCustom, calls=%fused_computation.clone.1 | custom fusion | bytes 8389120 | tf_op jit(solution)/shard_map/while/body/eval_jaxpr/gather | solution.py:41
  220.1 0.1 dynamic_slice.45
  220.2 7.6 %broadcast_select_fusion.2 = f32[64,128,256]{2,1,0:T(8,128)} fusion(pred[64]{0:T(512)(128)(4,1)S(1)} %dynamic_slice.45, bf16[64,128,256]{2,1,0:T(8,128)(2,1)} %gather_fusion, bf16[192,128,128]{2,1,0:T(8,128)(2,1)} %get-tuple-element.268, s32[]{:T(128)S(6)} %select_n.61), kind=kOutput, calls=%fused_computation.2.clone.1 | convolution fusion | flops 538968064 | bytes 14680132 | tf_op jit(solution)/shard_map/while/body/eval_jaxpr/kab,kaf->kbf/dot_general | solution.py:42
  227.8 19.6 %scatter_fusion = f32[64,128,256]{2,1,0:T(8,128)} fusion(f32[64,128,256]{2,1,0:T(8,128)} %get-tuple-element.253, s32[64]{0:T(128)S(1)} %get-tuple-element.238, f32[64,128,256]{2,1,0:T(8,128)} %broadcast_select_fusion.2), kind=kCustom, calls=%fused_computation.1.clone.1 | custom fusion | flops 2097152 | bytes 25166080 | tf_op jit(solution)/shard_map/while/body/eval_jaxpr/scatter-add | solution.py:44
  247.3 0.1 compare_select_fusion.4
  247.4 5.3 %gather_fusion = bf16[64,128,256]{2,1,0:T(8,128)(2,1)} fusion(bf16[128,128,4,256]{3,1,2,0:T(8,128)(2,1)} %get-tuple-element.271, s32[64]{0:T(128)S(1)} %get-tuple-element.239), kind=kCustom, calls=%fused_computation.clone.1 | custom fusion | bytes 8389120 | tf_op jit(solution)/shard_map/while/body/eval_jaxpr/gather | solution.py:41
  252.7 0.1 dynamic_slice.45
  252.8 7.6 %broadcast_select_fusion.2 = f32[64,128,256]{2,1,0:T(8,128)} fusion(pred[64]{0:T(512)(128)(4,1)S(1)} %dynamic_slice.45, bf16[64,128,256]{2,1,0:T(8,128)(2,1)} %gather_fusion, bf16[192,128,128]{2,1,0:T(8,128)(2,1)} %get-tuple-element.268, s32[]{:T(128)S(6)} %select_n.61), kind=kOutput, calls=%fused_computation.2.clone.1 | convolution fusion | flops 538968064 | bytes 14680132 | tf_op jit(solution)/shard_map/while/body/eval_jaxpr/kab,kaf->kbf/dot_general | solution.py:42
  260.3 19.4 %scatter_fusion = f32[64,128,256]{2,1,0:T(8,128)} fusion(f32[64,128,256]{2,1,0:T(8,128)} %get-tuple-element.253, s32[64]{0:T(128)S(1)} %get-tuple-element.238, f32[64,128,256]{2,1,0:T(8,128)} %broadcast_select_fusion.2), kind=kCustom, calls=%fused_computation.1.clone.1 | custom fusion | flops 2097152 | bytes 25166080 | tf_op jit(solution)/shard_map/while/body/eval_jaxpr/scatter-add | solution.py:44
  279.7 0.0 copy-start.1
  279.7 6.0 %convert_element_type.17 = bf16[64,128,256]{2,1,0:T(8,128)(2,1)} convert(f32[64,128,256]{2,1,0:T(8,128)} %get-tuple-element.144) | non-fusion elementwise | flops 2097152 | bytes 12582912 | tf_op jit(solution)/shard_map/convert_element_type | solution.py:48
  285.7 0.0 reduce-scatter.2.cloned.1.call-update
  285.8 38.0 %reduce-scatter.2.cloned.1.call-done = bf16[1024,256]{1,0:T(8,128)(2,1)} async-done(((bf16[8192,256]{1,0:T(8,128)(2,1)}), bf16[1024,256]{1,0:T(8,128)(2,1)}) %reduce-scatter.2.cloned.1.call-update) | async-done | bytes 524304 | tf_op jit(solution)/shard_map/reduce_scatter | solution.py:47
  323.8 2.1 convert_element_type.19
  325.9 0.0 copy-done.1
  (1 shorter events, 0.0 us)
Async XLA Ops:
  6.5 76.1 %copy-start = (bf16[4,256,256]{2,1,0:T(8,128)(2,1)S(1)}, bf16[4,256,256]{2,1,0:T(8,128)(2,1)}, u32[]{:S(2)}) copy-start(bf16[4,256,256]{2,1,0:T(8,128)(2,1)} %param.9) | copy-start | bytes 1572868
  6.5 76.1 %all-gather.2.cloned.1.call-start = ((), (), s32[]{:S(2)}) async-start(), calls=%async_computation.1 | async-start | bytes 8912896 | tf_op jit(solution)/shard_map/all_gather | solution.py:18
  7.3 316.5 %reduce-scatter.2.cloned.1.call-start = ((), (), s32[]{:S(2)}) async-start(), calls=%async_computation.2 | async-start | bytes 4718592 | tf_op jit(solution)/shard_map/reduce_scatter | solution.py:47
  177.9 4.2 %copy-start.2 = (s32[192]{0:T(256)S(1)}, s32[192]{0:T(256)}, u32[]{:S(2)}) copy-start(s32[192]{0:T(256)} %param.12) | copy-start | bytes 2308
  177.9 4.2 %copy-start.3 = (s32[192]{0:T(256)S(1)}, s32[192]{0:T(256)}, u32[]{:S(2)}) copy-start(s32[192]{0:T(256)} %param.11) | copy-start | bytes 2308
  279.7 46.1 %copy-start.1 = (bf16[4,256,256]{2,1,0:T(8,128)(2,1)S(1)}, bf16[4,256,256]{2,1,0:T(8,128)(2,1)}, u32[]{:S(2)}) copy-start(bf16[4,256,256]{2,1,0:T(8,128)(2,1)} %param.9) | copy-start | bytes 1572868
Sparse Core Ops, SparseCore 0:
  9.5 73.1 all-gather.1
  285.9 37.8 reduce-scatter.1
where the time goes:
time: 335 us; the launch traced here: 333 us
  waiting for transfers between devices  112 us (33%)
  local copies, waits for them, and re-layouts  98.6 us (29%)
  other arithmetic  68.4 us (20%)
  matrix products  40.1 us (12%)
  between operations  13.4 us (4%)
    all_gather x1, waiting for transfers between devices, per_device(): lax.all_gather(grad_out, 'col', axis=0, tiled=True)  73.3 us
    scatter-add x3, other arithmetic, step(): return partial_value.at[col_part].add(term)  58.6 us
    reshape x1, local copies, waits for them, and re-layouts, per_device(): table = gathered.reshape(ncols * owned, blk, kinds, feat)  54.7 us
    reduce_scatter x1, waiting for transfers between devices, per_device(): lax.psum_scatter(partial_value.reshape(nrows * owned * blk, feat).astype(...  38 us
    while x1, local copies, waits for them, and re-layouts, per_device(): partial_value = lax.fori_loop(0, groups, step, partial_start)  23 us
    dot_general x3, matrix products, step(): jnp.einsum('kab,kaf->kbf', adj_part, picked, preferred_element_type=jnp.f...  22.7 us
    dot_general x1, matrix products, per_device(): jnp.dot(lax.all_gather(grad_out, 'col', axis=0, tiled=True), wcat, prefer...  17.5 us
    gather x3, local copies, waits for them, and re-layouts, step(): picked = table[slot_part, :, kind_part, :]  15.9 us
  transfers between devices with their start and end apart: 2, of which 2 were waited for; matrix products, arithmetic and copies ran while one was open for 1% of the time, Pallas kernels for 0%

commit v1 on v0

--- a/solution.py
+++ b/solution.py
@@ -3,6 +3,31 @@
 import jax.numpy as jnp
 from jax import lax
 from jax.sharding import PartitionSpec as P
+
+
+def reach_packet_by_axis(local_array, net_axis):
+    met_up = lax.psum(1, net_axis)
+    mixed_arr, next_value, arr_out = (met_up, lax.axis_index(net_axis), local_array.shape[0])
+    series = [k * mixed_arr if p == 0 else k for p, k in enumerate(local_array.shape)]
+    tall = lax.dynamic_update_slice_in_dim(
+        jnp.zeros(series, local_array.dtype), local_array, next_value * arr_out, axis=0
+    )
+    after = v_now = local_array
+    b = 1
+    while b < mixed_arr // 2 + 1:
+        after = lax.ppermute(after, net_axis, [(p, (p + 1) % mixed_arr) for p in range(mixed_arr)])
+        tall = lax.dynamic_update_slice_in_dim(
+            tall, after, (next_value - b) % mixed_arr * arr_out, axis=0
+        )
+        if 2 * b < mixed_arr:
+            v_now = lax.ppermute(
+                v_now, net_axis, [(p, (p - 1) % mixed_arr) for p in range(mixed_arr)]
+            )
+            tall = lax.dynamic_update_slice_in_dim(
+                tall, v_now, (next_value + b) % mixed_arr * arr_out, axis=0
+            )
+        b = b + 1
+    return tall
 
 
 def per_device(grad_out, rel_weight, adjacency, block_row, block_col, type_count):
@@ -15,9 +40,7 @@
     slots_total = adjacency.shape[0]
     wcat = jnp.transpose(rel_weight, (2, 0, 1)).reshape(feat, kinds * feat)
     gathered = jnp.dot(
-        lax.all_gather(grad_out, "col", axis=0, tiled=True),
-        wcat,
-        preferred_element_type=jnp.float32,
+        reach_packet_by_axis(grad_out, "col"), wcat, preferred_element_type=jnp.float32
     ).astype(jnp.bfloat16)
     table = gathered.reshape(ncols * owned, blk, kinds, feat)
     ends = jnp.cumsum(type_count)

time: 335 us -> 373 us (1.11)
  starting transfers between devices: 0.04 us -> 37.5 us
  local copies, waits for them, and re-layouts: 98.6 us -> 122 us
  waiting for transfers between devices: 112 us -> 89.3 us
    all_gather x1 -> x0, waiting for transfers between devices: 73.3 us -> none  [per_device(): lax.all_gather(grad_out, 'col', axis=0, tiled=True)]
    ppermute x0 -> x15, waiting for transfers between devices: none -> 54.2 us  [the longest x8 53.8 us: reach_packet_by_axis(): lax.ppermute(after, net_axis, [(p, (p + 1) % mixed_arr) for p in range(mi...]
    ppermute x0 -> x15, starting transfers between devices: none -> 37.5 us  [the longest x7 35.9 us: reach_packet_by_axis(): lax.ppermute(v_now, net_axis, [(p, (p - 1) % mixed_arr) for p in range(mi...]
    dynamic_update_slice x0 -> x16, local copies, waits for them, and re-layouts: none -> 19.7 us  [the longest x8 9.83 us: reach_packet_by_axis(): lax.dynamic_update_slice_in_dim(tall, after, (next_value - b) % mixed_arr...]
  transfers between devices with their start and end apart: 2 -> 16, of which waited for: 2 -> 9; matrix products, arithmetic and copies ran while one was open for 1% -> 7% of each run, Pallas kernels for 0% -> 0%
where the time goes in v1:
time: 373 us; the launch traced here: 371 us
  local copies, waits for them, and re-layouts  122 us (33%)
  waiting for transfers between devices  89.3 us (24%)
  other arithmetic  68.4 us (18%)
  matrix products  40.2 us (11%)
  starting transfers between devices  37.5 us (10%)
  between operations  13.7 us (4%)
    scatter-add x3, other arithmetic, step(): return partial_value.at[col_part].add(term)  58.4 us
    reshape x1, local copies, waits for them, and re-layouts, per_device(): table = gathered.reshape(ncols * owned, blk, kinds, feat)  54.7 us
    ppermute x8, waiting for transfers between devices, reach_packet_by_axis(): lax.ppermute(after, net_axis, [(p, (p + 1) % mixed_arr) for p in range(mi...  53.8 us
    ppermute x7, starting transfers between devices, reach_packet_by_axis(): lax.ppermute(v_now, net_axis, [(p, (p - 1) % mixed_arr) for p in range(mi...  35.9 us
    reduce_scatter x1, waiting for transfers between devices, per_device(): lax.psum_scatter(partial_value.reshape(nrows * owned * blk, feat).astype(...  35.1 us
    while x1, local copies, waits for them, and re-layouts, per_device(): partial_value = lax.fori_loop(0, groups, step, partial_start)  23 us
    dot_general x3, matrix products, step(): jnp.einsum('kab,kaf->kbf', adj_part, picked, preferred_element_type=jnp.f...  22.7 us
    dot_general x1, matrix products, per_device(): jnp.dot(reach_packet_by_axis(grad_out, 'col'), wcat, preferred_element_ty...  17.5 us
  transfers between devices with their start and end apart: 16, of which 9 were waited for; matrix products, arithmetic and copies ran while one was open for 7% of the time, Pallas kernels for 0%

profile of v1, /device:TPU:0, one launch (start us, length us, event | category | flops | bytes accessed | tf_op | source)
XLA Modules:
  0.0 370.9 jit_solution(16858302423752766840)
XLA Ops:
  6.5 1.6 collective-permute-start
  8.1 3.8 %collective-permute-start.1 = (bf16[1024,256]{1,0:T(8,128)(2,1)}, bf16[1024,256]{1,0:T(8,128)(2,1)S(1)}, u32[]{:S(2)}, u32[]{:S(2)}) collective-permute-start(bf16[1024,256]{1,0:T(8,128)(2,1)} %param.8), channel_id=1, source_target_pairs={{0,15},{1,0},{2,1},{3,2},{4,3},{5,4},{6,5},{7,6},{8,7},{9,8},{10,9... | collective-permute-start | bytes 1572872 | tf_op jit(solution)/shard_map/ppermute | solution.py:23
  11.9 12.1 %collective-permute-done = bf16[1024,256]{1,0:T(8,128)(2,1)S(1)} collective-permute-done((bf16[1024,256]{1,0:T(8,128)(2,1)}, bf16[1024,256]{1,0:T(8,128)(2,1)S(1)}, u32[]{:S(2)}, u32[]{:S(2)}) %collective-permute-start) | collective-permute-done | bytes 524320 | tf_op jit(solution)/shard_map/ppermute | solution.py:18
  24.0 5.3 %collective-permute-start.3 = (bf16[1024,256]{1,0:T(8,128)(2,1)S(1)}, bf16[1024,256]{1,0:T(8,128)(2,1)S(1)}, u32[]{:S(2)}, u32[]{:S(2)}) collective-permute-start(bf16[1024,256]{1,0:T(8,128)(2,1)S(1)} %collective-permute-done.1), channel_id=1, source_target_pairs={{0,15},{1,0},{2,1},{3,2},{4,3},{5,4},{6,5},{7,6},{8,7},{9,8},{10,9... | collective-permute-start | bytes 1572872 | tf_op jit(solution)/shard_map/ppermute | solution.py:23
  29.4 11.1 %collective-permute-done.2 = bf16[1024,256]{1,0:T(8,128)(2,1)S(1)} collective-permute-done((bf16[1024,256]{1,0:T(8,128)(2,1)S(1)}, bf16[1024,256]{1,0:T(8,128)(2,1)S(1)}, u32[]{:S(2)}, u32[]{:S(2)}) %collective-permute-start.2) | collective-permute-done | bytes 524320 | tf_op jit(solution)/shard_map/ppermute | solution.py:18
  40.5 5.3 %collective-permute-start.5 = (bf16[1024,256]{1,0:T(8,128)(2,1)S(1)}, bf16[1024,256]{1,0:T(8,128)(2,1)S(1)}, u32[]{:S(2)}, u32[]{:S(2)}) collective-permute-start(bf16[1024,256]{1,0:T(8,128)(2,1)S(1)} %collective-permute-done.3), channel_id=1, source_target_pairs={{0,15},{1,0},{2,1},{3,2},{4,3},{5,4},{6,5},{7,6},{8,7},{9,8},{10,9... | collective-permute-start | bytes 1572872 | tf_op jit(solution)/shard_map/ppermute | solution.py:23
  45.8 10.2 %collective-permute-done.4 = bf16[1024,256]{1,0:T(8,128)(2,1)S(1)} collective-permute-done((bf16[1024,256]{1,0:T(8,128)(2,1)S(1)}, bf16[1024,256]{1,0:T(8,128)(2,1)S(1)}, u32[]{:S(2)}, u32[]{:S(2)}) %collective-permute-start.4) | collective-permute-done | bytes 524320 | tf_op jit(solution)/shard_map/ppermute | solution.py:18
  56.0 5.3 %collective-permute-start.7 = (bf16[1024,256]{1,0:T(8,128)(2,1)S(1)}, bf16[1024,256]{1,0:T(8,128)(2,1)}, u32[]{:S(2)}, u32[]{:S(2)}) collective-permute-start(bf16[1024,256]{1,0:T(8,128)(2,1)S(1)} %collective-permute-done.5), channel_id=1, source_target_pairs={{0,15},{1,0},{2,1},{3,2},{4,3},{5,4},{6,5},{7,6},{8,7},{9,8},{10,9... | collective-permute-start | bytes 1572872 | tf_op jit(solution)/shard_map/ppermute | solution.py:23
  61.3 9.5 %collective-permute-done.6 = bf16[1024,256]{1,0:T(8,128)(2,1)} collective-permute-done((bf16[1024,256]{1,0:T(8,128)(2,1)S(1)}, bf16[1024,256]{1,0:T(8,128)(2,1)}, u32[]{:S(2)}, u32[]{:S(2)}) %collective-permute-start.6) | collective-permute-done | bytes 524320 | tf_op jit(solution)/shard_map/ppermute | solution.py:18
  70.8 0.8 reduce-window.4
  71.7 5.4 %collective-permute-start.9 = (bf16[1024,256]{1,0:T(8,128)(2,1)}, bf16[1024,256]{1,0:T(8,128)(2,1)}, u32[]{:S(2)}, u32[]{:S(2)}) collective-permute-start(bf16[1024,256]{1,0:T(8,128)(2,1)} %collective-permute-done.7), channel_id=1, source_target_pairs={{0,15},{1,0},{2,1},{3,2},{4,3},{5,4},{6,5},{7,6},{8,7},{9,8},{10,9... | collective-permute-start | bytes 1572872 | tf_op jit(solution)/shard_map/ppermute | solution.py:23
  77.1 3.7 broadcast_in_dim.57
  80.8 0.8 constant_dynamic-update-slice_fusion.15
  82.3 2.7 collective-permute-done.8
  85.9 0.9 constant_dynamic-update-slice_fusion.14
  86.8 1.9 constant_dynamic-update-slice_fusion.13
  88.7 1.9 constant_dynamic-update-slice_fusion.12
  90.5 5.3 %collective-permute-start.11 = (bf16[1024,256]{1,0:T(8,128)(2,1)}, bf16[1024,256]{1,0:T(8,128)(2,1)S(1)}, u32[]{:S(2)}, u32[]{:S(2)}) collective-permute-start(bf16[1024,256]{1,0:T(8,128)(2,1)} %collective-permute-done.9), channel_id=1, source_target_pairs={{0,15},{1,0},{2,1},{3,2},{4,3},{5,4},{6,5},{7,6},{8,7},{9,8},{10,9... | collective-permute-start | bytes 1572872 | tf_op jit(solution)/shard_map/ppermute | solution.py:23
  95.8 0.8 constant_dynamic-update-slice_fusion.11
  96.7 1.5 collective-permute-done.10
  99.8 1.9 constant_dynamic-update-slice_fusion.8
  101.7 1.9 constant_dynamic-update-slice_fusion.7
  103.6 5.4 %collective-permute-start.13 = (bf16[1024,256]{1,0:T(8,128)(2,1)S(1)}, bf16[1024,256]{1,0:T(8,128)(2,1)S(1)}, u32[]{:S(2)}, u32[]{:S(2)}) collective-permute-start(bf16[1024,256]{1,0:T(8,128)(2,1)S(1)} %collective-permute-done.11), channel_id=1, source_target_pairs={{0,15},{1,0},{2,1},{3,2},{4,3},{5,4},{6,5},{7,6},{8,7},{9,8},{10,9... | collective-permute-start | bytes 1572872 | tf_op jit(solution)/shard_map/ppermute | solution.py:23
  108.9 1.9 constant_dynamic-update-slice_fusion.6
  110.8 1.9 constant_dynamic-update-slice_fusion.5
  112.7 0.8 constant_dynamic-update-slice_fusion.4
  113.5 0.9 constant_dynamic-update-slice_fusion.3
  114.4 0.9 constant_dynamic-update-slice_fusion.2
  115.6 0.8 constant_dynamic-update-slice_fusion.1
  116.5 6.8 %collective-permute-done.14 = bf16[1024,256]{1,0:T(8,128)(2,1)S(1)} collective-permute-done((bf16[1024,256]{1,0:T(8,128)(2,1)S(1)}, bf16[1024,256]{1,0:T(8,128)(2,1)S(1)}, u32[]{:S(2)}, u32[]{:S(2)}) %collective-permute-start.14) | collective-permute-done | bytes 524320 | tf_op jit(solution)/shard_map/ppermute | solution.py:18
  123.3 0.8 constant_dynamic-update-slice_fusion
  124.1 17.5 %convolution_convert_fusion = bf16[16384,1024]{1,0:T(8,128)(2,1)} fusion(bf16[16384,256]{1,0:T(8,128)(2,1)} %constant_dynamic-update-slice_fusion, bf16[256,1024]{0,1:T(8,128)(2,1)S(1)} %bitcast.12), kind=kOutput, calls=%fused_computation.13 | convolution fusion | flops 8606711808 | bytes 42467328 | tf_op jit(solution)/shard_map/dot_general | solution.py:42
  141.6 54.7 %reshape.19 = bf16[128,128,4,256]{3,2,1,0:T(4,128)(2,1)} reshape(bf16[16384,1024]{1,0:T(8,128)(2,1)} %convolution_convert_fusion) | data formatting | bytes 67108864 | tf_op jit(solution)/shard_map/reshape | solution.py:45
  196.3 23.0 %copy.12 = bf16[128,128,4,256]{3,1,2,0:T(8,128)(2,1)} copy(bf16[128,128,4,256]{3,2,1,0:T(4,128)(2,1)} %reshape.19) | data formatting | bytes 67108864 | tf_op jit(solution)/shard_map/while | solution.py:69
  219.4 4.2 %broadcast_in_dim.56 = f32[64,128,256]{2,1,0:T(8,128)} broadcast(f32[]{:T(128)} %constant.143.clone.1), dimensions={} | broadcast | bytes 8388612 | tf_op jit(solution)/shard_map/broadcast_in_dim | solution.py:55
  223.6 97.2 %while.13 = (s32[]{:T(128)}, f32[64,128,256]{2,1,0:T(8,128)}, s32[192]{0:T(256)S(1)}, pred[192]{0:T(512)(128)(4,1)S(1)}, bf16[192,128,128]{2,1,0:T(8,128)(2,1)},...) while((s32[]{:T(128)}, f32[64,128,256]{2,1,0:T(8,128)}, ...), condition=%wide.region_4.5_spmd, body=%wide.region_2.4_spmd.sunk | while | flops 541066112 | bytes 48236912 | solution.py:69
  223.7 5.1 %gather_fusion = bf16[64,128,256]{2,1,0:T(8,128)(2,1)} fusion(bf16[128,128,4,256]{3,1,2,0:T(8,128)(2,1)} %get-tuple-element.271, s32[64]{0:T(128)S(1)} %get-tuple-element.239), kind=kCustom, calls=%fused_computation.clone.1 | custom fusion | bytes 8389120 | tf_op jit(solution)/shard_map/while/body/eval_jaxpr/gather | solution.py:64
  228.8 7.6 %broadcast_select_fusion.2 = f32[64,128,256]{2,1,0:T(8,128)} fusion(pred[64]{0:T(512)(128)(4,1)S(1)} %dynamic_slice.45, bf16[64,128,256]{2,1,0:T(8,128)(2,1)} %gather_fusion, bf16[192,128,128]{2,1,0:T(8,128)(2,1)} %get-tuple-element.268, s32[]{:T(128)S(6)} %select_n.203), kind=kOutput, calls=%fused_computation.2.clone.1 | convolution fusion | flops 538968064 | bytes 14680132 | tf_op jit(solution)/shard_map/while/body/eval_jaxpr/kab,kaf->kbf/dot_general | solution.py:65
  236.4 19.5 %scatter_fusion = f32[64,128,256]{2,1,0:T(8,128)} fusion(f32[64,128,256]{2,1,0:T(8,128)} %get-tuple-element.253, s32[64]{0:T(128)S(1)} %get-tuple-element.238, f32[64,128,256]{2,1,0:T(8,128)} %broadcast_select_fusion.2), kind=kCustom, calls=%fused_computation.1.clone.1 | custom fusion | flops 2097152 | bytes 25166080 | tf_op jit(solution)/shard_map/while/body/eval_jaxpr/scatter-add | solution.py:67
  255.9 5.4 %gather_fusion = bf16[64,128,256]{2,1,0:T(8,128)(2,1)} fusion(bf16[128,128,4,256]{3,1,2,0:T(8,128)(2,1)} %get-tuple-element.271, s32[64]{0:T(128)S(1)} %get-tuple-element.239), kind=kCustom, calls=%fused_computation.clone.1 | custom fusion | bytes 8389120 | tf_op jit(solution)/shard_map/while/body/eval_jaxpr/gather | solution.py:64
  261.4 7.6 %broadcast_select_fusion.2 = f32[64,128,256]{2,1,0:T(8,128)} fusion(pred[64]{0:T(512)(128)(4,1)S(1)} %dynamic_slice.45, bf16[64,128,256]{2,1,0:T(8,128)(2,1)} %gather_fusion, bf16[192,128,128]{2,1,0:T(8,128)(2,1)} %get-tuple-element.268, s32[]{:T(128)S(6)} %select_n.203), kind=kOutput, calls=%fused_computation.2.clone.1 | convolution fusion | flops 538968064 | bytes 14680132 | tf_op jit(solution)/shard_map/while/body/eval_jaxpr/kab,kaf->kbf/dot_general | solution.py:65
  269.0 19.6 %scatter_fusion = f32[64,128,256]{2,1,0:T(8,128)} fusion(f32[64,128,256]{2,1,0:T(8,128)} %get-tuple-element.253, s32[64]{0:T(128)S(1)} %get-tuple-element.238, f32[64,128,256]{2,1,0:T(8,128)} %broadcast_select_fusion.2), kind=kCustom, calls=%fused_computation.1.clone.1 | custom fusion | flops 2097152 | bytes 25166080 | tf_op jit(solution)/shard_map/while/body/eval_jaxpr/scatter-add | solution.py:67
  288.6 5.1 %gather_fusion = bf16[64,128,256]{2,1,0:T(8,128)(2,1)} fusion(bf16[128,128,4,256]{3,1,2,0:T(8,128)(2,1)} %get-tuple-element.271, s32[64]{0:T(128)S(1)} %get-tuple-element.239), kind=kCustom, calls=%fused_computation.clone.1 | custom fusion | bytes 8389120 | tf_op jit(solution)/shard_map/while/body/eval_jaxpr/gather | solution.py:64
  293.9 7.6 %broadcast_select_fusion.2 = f32[64,128,256]{2,1,0:T(8,128)} fusion(pred[64]{0:T(512)(128)(4,1)S(1)} %dynamic_slice.45, bf16[64,128,256]{2,1,0:T(8,128)(2,1)} %gather_fusion, bf16[192,128,128]{2,1,0:T(8,128)(2,1)} %get-tuple-element.268, s32[]{:T(128)S(6)} %select_n.203), kind=kOutput, calls=%fused_computation.2.clone.1 | convolution fusion | flops 538968064 | bytes 14680132 | tf_op jit(solution)/shard_map/while/body/eval_jaxpr/kab,kaf->kbf/dot_general | solution.py:65
  301.4 19.4 %scatter_fusion = f32[64,128,256]{2,1,0:T(8,128)} fusion(f32[64,128,256]{2,1,0:T(8,128)} %get-tuple-element.253, s32[64]{0:T(128)S(1)} %get-tuple-element.238, f32[64,128,256]{2,1,0:T(8,128)} %broadcast_select_fusion.2), kind=kCustom, calls=%fused_computation.1.clone.1 | custom fusion | flops 2097152 | bytes 25166080 | tf_op jit(solution)/shard_map/while/body/eval_jaxpr/scatter-add | solution.py:67
  320.8 6.0 %convert_element_type.17 = bf16[64,128,256]{2,1,0:T(8,128)(2,1)} convert(f32[64,128,256]{2,1,0:T(8,128)} %get-tuple-element.144) | non-fusion elementwise | flops 2097152 | bytes 12582912 | tf_op jit(solution)/shard_map/convert_element_type | solution.py:71
  326.8 35.1 %reduce-scatter.2.cloned.1.call-done = bf16[1024,256]{1,0:T(8,128)(2,1)} async-done(((bf16[8192,256]{1,0:T(8,128)(2,1)}), bf16[1024,256]{1,0:T(8,128)(2,1)}) %reduce-scatter.2.cloned.1.call-update) | async-done | bytes 524304 | tf_op jit(solution)/shard_map/reduce_scatter | solution.py:70
  362.0 2.1 convert_element_type.19
  (43 shorter events, 4.0 us)
Async XLA Ops:
  6.5 117.6 %copy-start = (bf16[4,256,256]{2,1,0:T(8,128)(2,1)S(1)}, bf16[4,256,256]{2,1,0:T(8,128)(2,1)}, u32[]{:S(2)}) copy-start(bf16[4,256,256]{2,1,0:T(8,128)(2,1)} %param.9) | copy-start | bytes 1572868
  6.5 74.3 %copy-start.2 = (bf16[1024,256]{1,0:T(8,128)(2,1)S(1)}, bf16[1024,256]{1,0:T(8,128)(2,1)}, u32[]{:S(2)}) copy-start(bf16[1024,256]{1,0:T(8,128)(2,1)} %param.8) | copy-start | bytes 1572868
  6.5 355.4 %reduce-scatter.2.cloned.1.call-start = ((), (), s32[]{:S(2)}) async-start(), calls=%async_computation.1 | async-start | bytes 4718592 | tf_op jit(solution)/shard_map/reduce_scatter | solution.py:70
  6.5 17.5 %collective-permute-start = (bf16[1024,256]{1,0:T(8,128)(2,1)}, bf16[1024,256]{1,0:T(8,128)(2,1)S(1)}, u32[]{:S(2)}, u32[]{:S(2)}) collective-permute-start(bf16[1024,256]{1,0:T(8,128)(2,1)} %param.8), channel_id=1, source_target_pairs={{0,1},{1,2},{2,3},{3,4},{4,5},{5,6},{6,7},{7,8},{8,9},{9,10},{10,1... | collective-permute-start | bytes 1572872 | tf_op jit(solution)/shard_map/ppermute | solution.py:18
  8.1 15.9 %collective-permute-start.1 = (bf16[1024,256]{1,0:T(8,128)(2,1)}, bf16[1024,256]{1,0:T(8,128)(2,1)S(1)}, u32[]{:S(2)}, u32[]{:S(2)}) collective-permute-start(bf16[1024,256]{1,0:T(8,128)(2,1)} %param.8), channel_id=1, source_target_pairs={{0,15},{1,0},{2,1},{3,2},{4,3},{5,4},{6,5},{7,6},{8,7},{9,8},{10,9... | collective-permute-start | bytes 1572872 | tf_op jit(solution)/shard_map/ppermute | solution.py:23
  24.0 16.4 %collective-permute-start.2 = (bf16[1024,256]{1,0:T(8,128)(2,1)S(1)}, bf16[1024,256]{1,0:T(8,128)(2,1)S(1)}, u32[]{:S(2)}, u32[]{:S(2)}) collective-permute-start(bf16[1024,256]{1,0:T(8,128)(2,1)S(1)} %collective-permute-done), channel_id=1, source_target_pairs={{0,1},{1,2},{2,3},{3,4},{4,5},{5,6},{6,7},{7,8},{8,9},{9,10},{10,1... | collective-permute-start | bytes 1572872 | tf_op jit(solution)/shard_map/ppermute | solution.py:18
  24.0 16.4 %copy-start.3 = (bf16[1024,256]{1,0:T(8,128)(2,1)}, bf16[1024,256]{1,0:T(8,128)(2,1)S(1)}, u32[]{:S(2)}) copy-start(bf16[1024,256]{1,0:T(8,128)(2,1)S(1)} %collective-permute-done.1) | copy-start | bytes 1572868
  24.0 16.4 %collective-permute-start.3 = (bf16[1024,256]{1,0:T(8,128)(2,1)S(1)}, bf16[1024,256]{1,0:T(8,128)(2,1)S(1)}, u32[]{:S(2)}, u32[]{:S(2)}) collective-permute-start(bf16[1024,256]{1,0:T(8,128)(2,1)S(1)} %collective-permute-done.1), channel_id=1, source_target_pairs={{0,15},{1,0},{2,1},{3,2},{4,3},{5,4},{6,5},{7,6},{8,7},{9,8},{10,9... | collective-permute-start | bytes 1572872 | tf_op jit(solution)/shard_map/ppermute | solution.py:23
  40.4 30.4 %copy-start.4 = (bf16[1024,256]{1,0:T(8,128)(2,1)}, bf16[1024,256]{1,0:T(8,128)(2,1)S(1)}, u32[]{:S(2)}) copy-start(bf16[1024,256]{1,0:T(8,128)(2,1)S(1)} %collective-permute-done.2) | copy-start | bytes 1572868
  40.4 15.6 %collective-permute-start.4 = (bf16[1024,256]{1,0:T(8,128)(2,1)S(1)}, bf16[1024,256]{1,0:T(8,128)(2,1)S(1)}, u32[]{:S(2)}, u32[]{:S(2)}) collective-permute-start(bf16[1024,256]{1,0:T(8,128)(2,1)S(1)} %collective-permute-done.2), channel_id=1, source_target_pairs={{0,1},{1,2},{2,3},{3,4},{4,5},{5,6},{6,7},{7,8},{8,9},{9,10},{10,1... | collective-permute-start | bytes 1572872 | tf_op jit(solution)/shard_map/ppermute | solution.py:18
  40.5 15.5 %collective-permute-start.5 = (bf16[1024,256]{1,0:T(8,128)(2,1)S(1)}, bf16[1024,256]{1,0:T(8,128)(2,1)S(1)}, u32[]{:S(2)}, u32[]{:S(2)}) collective-permute-start(bf16[1024,256]{1,0:T(8,128)(2,1)S(1)} %collective-permute-done.3), channel_id=1, source_target_pairs={{0,15},{1,0},{2,1},{3,2},{4,3},{5,4},{6,5},{7,6},{8,7},{9,8},{10,9... | collective-permute-start | bytes 1572872 | tf_op jit(solution)/shard_map/ppermute | solution.py:23
  56.0 14.8 %collective-permute-start.6 = (bf16[1024,256]{1,0:T(8,128)(2,1)S(1)}, bf16[1024,256]{1,0:T(8,128)(2,1)}, u32[]{:S(2)}, u32[]{:S(2)}) collective-permute-start(bf16[1024,256]{1,0:T(8,128)(2,1)S(1)} %collective-permute-done.4), channel_id=1, source_target_pairs={{0,1},{1,2},{2,3},{3,4},{4,5},{5,6},{6,7},{7,8},{8,9},{9,10},{10,1... | collective-permute-start | bytes 1572872 | tf_op jit(solution)/shard_map/ppermute | solution.py:18
  56.0 15.7 %collective-permute-start.7 = (bf16[1024,256]{1,0:T(8,128)(2,1)S(1)}, bf16[1024,256]{1,0:T(8,128)(2,1)}, u32[]{:S(2)}, u32[]{:S(2)}) collective-permute-start(bf16[1024,256]{1,0:T(8,128)(2,1)S(1)} %collective-permute-done.5), channel_id=1, source_target_pairs={{0,15},{1,0},{2,1},{3,2},{4,3},{5,4},{6,5},{7,6},{8,7},{9,8},{10,9... | collective-permute-start | bytes 1572872 | tf_op jit(solution)/shard_map/ppermute | solution.py:23
  70.8 14.2 %collective-permute-start.8 = (bf16[1024,256]{1,0:T(8,128)(2,1)}, bf16[1024,256]{1,0:T(8,128)(2,1)}, u32[]{:S(2)}, u32[]{:S(2)}) collective-permute-start(bf16[1024,256]{1,0:T(8,128)(2,1)} %collective-permute-done.6), channel_id=1, source_target_pairs={{0,1},{1,2},{2,3},{3,4},{4,5},{5,6},{6,7},{7,8},{8,9},{9,10},{10,1... | collective-permute-start | bytes 1572872 | tf_op jit(solution)/shard_map/ppermute | solution.py:18
  71.7 18.8 %collective-permute-start.9 = (bf16[1024,256]{1,0:T(8,128)(2,1)}, bf16[1024,256]{1,0:T(8,128)(2,1)}, u32[]{:S(2)}, u32[]{:S(2)}) collective-permute-start(bf16[1024,256]{1,0:T(8,128)(2,1)} %collective-permute-done.7), channel_id=1, source_target_pairs={{0,15},{1,0},{2,1},{3,2},{4,3},{5,4},{6,5},{7,6},{8,7},{9,8},{10,9... | collective-permute-start | bytes 1572872 | tf_op jit(solution)/shard_map/ppermute | solution.py:23
  85.0 13.2 %collective-permute-start.10 = (bf16[1024,256]{1,0:T(8,128)(2,1)}, bf16[1024,256]{1,0:T(8,128)(2,1)S(1)}, u32[]{:S(2)}, u32[]{:S(2)}) collective-permute-start(bf16[1024,256]{1,0:T(8,128)(2,1)} %collective-permute-done.8), channel_id=1, source_target_pairs={{0,1},{1,2},{2,3},{3,4},{4,5},{5,6},{6,7},{7,8},{8,9},{9,10},{10,1... | collective-permute-start | bytes 1572872 | tf_op jit(solution)/shard_map/ppermute | solution.py:18
  90.5 13.0 %collective-permute-start.11 = (bf16[1024,256]{1,0:T(8,128)(2,1)}, bf16[1024,256]{1,0:T(8,128)(2,1)S(1)}, u32[]{:S(2)}, u32[]{:S(2)}) collective-permute-start(bf16[1024,256]{1,0:T(8,128)(2,1)} %collective-permute-done.9), channel_id=1, source_target_pairs={{0,15},{1,0},{2,1},{3,2},{4,3},{5,4},{6,5},{7,6},{8,7},{9,8},{10,9... | collective-permute-start | bytes 1572872 | tf_op jit(solution)/shard_map/ppermute | solution.py:23
  98.1 12.7 %collective-permute-start.12 = (bf16[1024,256]{1,0:T(8,128)(2,1)S(1)}, bf16[1024,256]{1,0:T(8,128)(2,1)S(1)}, u32[]{:S(2)}, u32[]{:S(2)}) collective-permute-start(bf16[1024,256]{1,0:T(8,128)(2,1)S(1)} %collective-permute-done.10), channel_id=1, source_target_pairs={{0,1},{1,2},{2,3},{3,4},{4,5},{5,6},{6,7},{7,8},{8,9},{9,10},{10,1... | collective-permute-start | bytes 1572872 | tf_op jit(solution)/shard_map/ppermute | solution.py:18
  103.6 12.1 %collective-permute-start.13 = (bf16[1024,256]{1,0:T(8,128)(2,1)S(1)}, bf16[1024,256]{1,0:T(8,128)(2,1)S(1)}, u32[]{:S(2)}, u32[]{:S(2)}) collective-permute-start(bf16[1024,256]{1,0:T(8,128)(2,1)S(1)} %collective-permute-done.11), channel_id=1, source_target_pairs={{0,15},{1,0},{2,1},{3,2},{4,3},{5,4},{6,5},{7,6},{8,7},{9,8},{10,9... | collective-permute-start | bytes 1572872 | tf_op jit(solution)/shard_map/ppermute | solution.py:23
  110.8 12.5 %collective-permute-start.14 = (bf16[1024,256]{1,0:T(8,128)(2,1)S(1)}, bf16[1024,256]{1,0:T(8,128)(2,1)S(1)}, u32[]{:S(2)}, u32[]{:S(2)}) collective-permute-start(bf16[1024,256]{1,0:T(8,128)(2,1)S(1)} %collective-permute-done.12), channel_id=1, source_target_pairs={{0,1},{1,2},{2,3},{3,4},{4,5},{5,6},{6,7},{7,8},{8,9},{9,10},{10,1... | collective-permute-start | bytes 1572872 | tf_op jit(solution)/shard_map/ppermute | solution.py:18
  219.3 4.2 %copy-start.5 = (s32[192]{0:T(256)S(1)}, s32[192]{0:T(256)}, u32[]{:S(2)}) copy-start(s32[192]{0:T(256)} %param.12) | copy-start | bytes 2308
  219.3 4.2 %copy-start.6 = (s32[192]{0:T(256)S(1)}, s32[192]{0:T(256)}, u32[]{:S(2)}) copy-start(s32[192]{0:T(256)} %param.11) | copy-start | bytes 2308
  320.8 43.3 %copy-start.1 = (bf16[4,256,256]{2,1,0:T(8,128)(2,1)S(1)}, bf16[4,256,256]{2,1,0:T(8,128)(2,1)}, u32[]{:S(2)}) copy-start(bf16[4,256,256]{2,1,0:T(8,128)(2,1)} %param.9) | copy-start | bytes 1572868
Sparse Core Ops, SparseCore 0:
  327.0 34.9 reduce-scatter.1
